TPU v7x, 32 devices: a whole 2x2x4 slice. The times are simulated.
32 devices in a mesh: gy: 8 (over y, x, core), gx: 4 (over z).
Axes of the slice: x: 2, y: 2, z: 4, core: 2. Of those that a mesh axis runs over, the one named last changes fastest.
Arguments:
- tracer: float32 [8, 1024, 1024], P(None, 'gy', 'gx'), may hold values from -6 to 6
- east_speed: float32 [8, 1024, 1024], P(None, 'gy', 'gx'), may hold values from -0.25 to 0.25
- north_speed: float32 [8, 1024, 1024], P(None, 'gy', 'gx'), may hold values from -0.25 to 0.25
- columns: int32 [1024, 1024], P('gy', 'gx'), may hold values from 0 to 8
- thickness: float32 [8], replicated, may hold values from 0.5 to 2
- surface_flux: float32 [1024, 1024], P('gy', 'gx'), may hold values from -6 to 6
- helm: float32 [1024, 1024], P('gy', 'gx'), may hold values from 0.2 to 4
Outputs:
- tracer_new: float32 [8, 1024, 1024], P(None, 'gy', 'gx')
- heights: float32 [1024, 1024], P('gy', 'gx')
Inputs may be any that keep to these rules, and one draw needn't show every extreme that they name: `columns`: ocean levels per column; 0 means land.
All inputs are finite; a program needn't handle non-finite values.
Results may differ from a plain program's by a relative error of at most 0.0001.
Values sent between devices are 32-bit elements; how exact they have to be, the bound alone decides.
A program may use at most 64 MiB of HBM per device.

v0:
```python
import jax
import jax.numpy as jnp
from jax import lax
from jax.sharding import PartitionSpec as P

TSTEPS = 2
ITERS = 3


def extended_2(array, sides, width, wrap):
    for axis, dim in sides:
        peers, length = (lax.axis_size(axis), array.shape[dim])
        up = [(i, (i + 1) % peers) for i in range(peers if wrap else peers - 1)]
        down = [(j, i) for i, j in up]
        last = lax.slice_in_dim(array, length - width, length, axis=dim)
        first = lax.slice_in_dim(array, 0, width, axis=dim)
        before = lax.ppermute(last, axis, up)
        after = lax.ppermute(first, axis, down)
        array = jnp.concatenate([before, array, after], axis=dim)
    return array


def upwind(speed, behind, ahead):
    return jnp.maximum(speed, 0.0) * behind + jnp.minimum(speed, 0.0) * ahead


def advect_block(extended, east_ext, north_ext, ocean_ext):
    centre = extended[:, 1:-1, 1:-1]
    open_east = ocean_ext[:, 1:-1, :-1] * ocean_ext[:, 1:-1, 1:]
    flux_east = open_east * upwind(
        east_ext[:, 1:-1, :-1], extended[:, 1:-1, :-1], extended[:, 1:-1, 1:]
    )
    open_north = ocean_ext[:, :-1, 1:-1] * ocean_ext[:, 1:, 1:-1]
    flux_north = open_north * upwind(
        north_ext[:, :-1, 1:-1], extended[:, :-1, 1:-1], extended[:, 1:, 1:-1]
    )
    return centre - (
        flux_east[:, :, 1:] - flux_east[:, :, :-1] + flux_north[:, 1:, :] - flux_north[:, :-1, :]
    )


def stencil(extended, wet_ext, diagonal_term):
    weighted = wet_ext * extended
    edges = weighted[1:-1, 2:] + weighted[1:-1, :-2] + weighted[2:, 1:-1] + weighted[:-2, 1:-1]
    corners = weighted[2:, 2:] + weighted[2:, :-2] + weighted[:-2, 2:] + weighted[:-2, :-2]
    return diagonal_term * extended[1:-1, 1:-1] - wet_ext[1:-1, 1:-1] * (edges + 0.5 * corners)


def wrap_columns(source):
    return jnp.concatenate([source[:, -1:], source, source[:, :1]], axis=1)


def solve(forcing, diagonal_term, apply_matrix, sum_all):
    heights = jnp.zeros_like(forcing)
    residual = forcing
    scaled = residual / diagonal_term
    applied = apply_matrix(scaled)
    product_now, curvature = sum_all((jnp.sum(residual * scaled), jnp.sum(applied * scaled)))
    step_size = product_now / curvature
    direction = scaled
    along = applied
    for iteration in range(ITERS):
        heights = heights + step_size * direction
        residual = residual - step_size * along
        if iteration + 1 < ITERS:
            scaled = residual / diagonal_term
            applied = apply_matrix(scaled)
            product_next, curvature = sum_all(
                (jnp.sum(residual * scaled), jnp.sum(applied * scaled))
            )
            factor = product_next / product_now
            step_size = product_next / (curvature - factor * product_next / step_size)
            direction = scaled + factor * direction
            along = applied + factor * along
            product_now = product_next
    return heights


def on_device(tracer, east_speed, north_speed, columns, thickness, surface_flux, helm):
    levels, rows_dev, cols_dev = tracer.shape
    depth = lax.broadcasted_iota(jnp.int32, tracer.shape, 0)
    ocean = (depth < columns[None]).astype(jnp.float32)
    stacked = jnp.stack([east_speed, north_speed, ocean])
    static_ext = extended_2(stacked, (("gy", 2), ("gx", 3)), 1, True)
    position = lax.axis_index("gy")
    last_row = lax.axis_size("gy") - 1
    row_ids = lax.broadcasted_iota(jnp.int32, (rows_dev + 2, 1), 0)
    closed = (row_ids == 0) & (position == 0) | (row_ids == rows_dev + 1) & (position == last_row)
    row_keep = jnp.where(closed, 0.0, 1.0).astype(jnp.float32)
    ocean_ext = static_ext[2] * row_keep[None]
    current = tracer
    for section_index in range(TSTEPS):
        extended = extended_2(current, (("gy", 1), ("gx", 2)), 1, True)
        current = advect_block(extended, static_ext[0], static_ext[1], ocean_ext)
    forcing = surface_flux + jnp.sum(thickness[:, None, None] * ocean * current, axis=0)
    band_rhs, band_helm, band_wet = (
        lax.all_gather(forcing, "gx", axis=1, tiled=True),
        lax.all_gather(helm, "gx", axis=1, tiled=True),
        lax.all_gather(ocean_ext[0, :, 1:-1], "gx", axis=1, tiled=True),
    )
    wet_wrapped = wrap_columns(band_wet)
    band_diagonal = 6.0 + band_helm

    def apply_band(source):
        rimmed = extended_2(source, (("gy", 0),), 1, False)
        return stencil(wrap_columns(rimmed), wet_wrapped, band_diagonal)

    def sum_band(values):
        return lax.psum(values, "gy")

    band_heights = solve(band_rhs, band_diagonal, apply_band, sum_band)
    heights = lax.dynamic_slice_in_dim(band_heights, lax.axis_index("gx") * cols_dev, cols_dev, 1)
    return (current, heights)


def solution(mesh):
    in_specs = (
        P(None, "gy", "gx"),
        P(None, "gy", "gx"),
        P(None, "gy", "gx"),
        P("gy", "gx"),
        P(),
        P("gy", "gx"),
        P("gy", "gx"),
    )
    out_specs = (P(None, "gy", "gx"), P("gy", "gx"))
    return jax.shard_map(
        on_device, mesh=mesh, in_specs=in_specs, out_specs=out_specs, check_vma=False
    )
```

profile of v0, /device:TPU:4, one launch (start us, length us, event | category | flops | bytes accessed | tf_op | source)
XLA Modules:
  0.0 213.6 jit_solution(6373276697639543300)
XLA Ops:
  3.0 2.6 %collective-permute-start.1 = (f32[3,8,1,256]{3,2,1,0:T(1,128)S(1)}, f32[3,8,1,256]{3,2,1,0:T(1,128)S(1)}, u32[]{:S(2)}, u32[]{:S(2)}) collective-permute-start(f32[3,8,1,256]{3,2,1,0:T(1,128)S(1)} %get-tuple-element.27), channel_id=1, source_target_pairs={{4,0},{8,4},{12,8},{16,12},{20,16},{24,20},{28,24},{0,28},{5,1},{9... | collective-permute-start | bytes 73736 | tf_op jit(solution)/shard_map/ppermute | solution.py:18
  5.7 2.6 %collective-permute-start.5 = (f32[8,1,256]{2,1,0:T(1,128)S(1)}, f32[8,1,256]{2,1,0:T(1,128)S(1)}, u32[]{:S(2)}, u32[]{:S(2)}) collective-permute-start(f32[8,1,256]{2,1,0:T(1,128)S(1)} %get-tuple-element.34), channel_id=1, source_target_pairs={{4,0},{8,4},{12,8},{16,12},{20,16},{24,20},{28,24},{0,28},{5,1},{9... | collective-permute-start | bytes 24584 | tf_op jit(solution)/shard_map/ppermute | solution.py:18
  8.3 15.8 %all_gather.10 = f32[128,1024]{1,0:T(8,128)S(1)} all-gather(f32[128,256]{1,0:T(8,128)S(1)} %copy-done.16), channel_id=1, replica_groups=mesh['gy'=8,'gx'=4] {'gx'}, dimensions={1}, use_global_device_ids=true | all-gather | bytes 655360 | tf_op jit(solution)/shard_map/all_gather | solution.py:98
  27.8 3.1 %collective-permute-start.7 = (f32[8,130,1]{1,0,2:T(8,128)S(1)}, f32[8,130,1]{1,0,2:T(8,128)S(1)}, u32[]{:S(2)}, u32[]{:S(2)}) collective-permute-start(f32[8,130,1]{1,0,2:T(8,128)S(1)} %copy.29), channel_id=1, source_target_pairs={{1,0},{2,1},{3,2},{0,3},{5,4},{6,5},{7,6},{4,7},{9,8},{10,9},{11,1... | collective-permute-start | bytes 12488 | tf_op jit(solution)/shard_map/ppermute | solution.py:18
  30.9 1.9 pad_maximum_fusion.1
  32.8 2.2 %fusion.35 = (f32[3,8,130,1]{3,2,1,0:T(8,128)}, f32[3,8,130,1]{3,2,1,0:T(8,128)}) fusion(f32[3,8,130,256]{3,2,1,0:T(8,128)S(1)} %pad_maximum_fusion.1), kind=kLoop, calls=%fused_computation.108 | loop fusion | bytes 49920 | tf_op jit(solution)/shard_map/slice | solution.py:15
  35.0 2.3 %copy.23 = f32[3,8,130,1]{2,1,3,0:T(8,128)S(1)} copy(f32[3,8,130,1]{3,2,1,0:T(8,128)} %get-tuple-element.24) | data formatting | bytes 24960 | tf_op jit(solution)/shard_map/slice | solution.py:15
  37.4 2.3 %copy.24 = f32[3,8,130,1]{2,1,3,0:T(8,128)S(1)} copy(f32[3,8,130,1]{3,2,1,0:T(8,128)} %get-tuple-element.25) | data formatting | bytes 24960 | tf_op jit(solution)/shard_map/slice | solution.py:16
  39.7 3.8 %collective-permute-start.3 = (f32[3,8,130,1]{2,1,3,0:T(8,128)S(1)}, f32[3,8,130,1]{2,1,3,0:T(8,128)S(1)}, u32[]{:S(2)}, u32[]{:S(2)}) collective-permute-start(f32[3,8,130,1]{2,1,3,0:T(8,128)S(1)} %copy.24), channel_id=1, source_target_pairs={{1,0},{2,1},{3,2},{0,3},{5,4},{6,5},{7,6},{4,7},{9,8},{10,9},{11,1... | collective-permute-start | bytes 37448 | tf_op jit(solution)/shard_map/ppermute | solution.py:18
  45.7 1.8 copy.25
  47.5 1.8 copy.26
  49.3 5.7 %pad_maximum_fusion = f32[3,8,130,258]{3,2,1,0:T(8,128)S(1)} fusion(f32[3,8,130,1]{3,2,1,0:T(8,128)} %copy.26, f32[3,8,1,256]{3,2,1,0:T(1,128)S(1)} %collective-permute-done.1, f32[1,8,128,256]{3,2,1,0:T(8,128)S(1)} %fusion.15, f32[1,8,128,256]{3,2,1,0:T(8,128)} %bitcast.24, f32[1,8,128,256]{3,2,1,0:T(8,128)} %bitcast.28, ...), kind=kLoop, calls=%fused_computation | loop fusion | flops 4829760 | bytes 6439680 | tf_op jit(solution)/shard_map/concatenate | solution.py:19
  59.3 2.6 %collective-permute-start.9 = (f32[8,1,256]{2,1,0:T(1,128)S(1)}, f32[8,1,256]{2,1,0:T(1,128)S(1)}, u32[]{:S(2)}, u32[]{:S(2)}) collective-permute-start(f32[8,1,256]{2,1,0:T(1,128)S(1)} %get-tuple-element.32), channel_id=1, source_target_pairs={{4,0},{8,4},{12,8},{16,12},{20,16},{24,20},{28,24},{0,28},{5,1},{9... | collective-permute-start | bytes 24584 | tf_op jit(solution)/shard_map/ppermute | solution.py:18
  62.0 16.8 %all-gather = f32[1,130,1024]{2,1,0:T(8,128)} all-gather(f32[1,130,256]{2,1,0:T(8,128)S(1)} %slice.340), channel_id=2, replica_groups=mesh['gy'=8,'gx'=4] {'gx'}, dimensions={2}, use_global_device_ids=true | all-gather | bytes 665600 | tf_op jit(solution)/shard_map/all_gather | solution.py:99
  82.9 4.0 %collective-permute-start.11 = (f32[8,130,1]{1,0,2:T(8,128)S(1)}, f32[8,130,1]{1,0,2:T(8,128)S(1)}, u32[]{:S(2)}, u32[]{:S(2)}) collective-permute-start(f32[8,130,1]{1,0,2:T(8,128)S(1)} %copy.33), channel_id=1, source_target_pairs={{1,0},{2,1},{3,2},{0,3},{5,4},{6,5},{7,6},{4,7},{9,8},{10,9},{11,1... | collective-permute-start | bytes 12488 | tf_op jit(solution)/shard_map/ppermute | solution.py:18
  86.9 3.4 %fusion.12 = f32[8,129,256]{2,1,0:T(8,128)} fusion(f32[8,128,256]{2,1,0:T(8,128)S(1)} %fusion.14, f32[8,1,256]{2,1,0:T(1,128)S(1)} %collective-permute-done.8, f32[8,1,256]{2,1,0:T(1,128)S(1)} %collective-permute-done.9, f32[8,130,258]{2,1,0:T(8,128)} %copy-done.6, f32[8,130,258]{2,1,0:T(8,128)S(1)} %fusion), kind=kLoop, calls=%fused_computation.38 | loop fusion | flops 2377728 | bytes 5292032 | tf_op jit(solution)/shard_map/mul | solution.py:34
  92.4 3.0 %fusion.3 = f32[8,128,257]{2,1,0:T(8,128)S(1)} fusion(f32[8,130,1]{2,1,0:T(8,128)} %copy.34, f32[8,1,256]{2,1,0:T(1,128)S(1)} %collective-permute-done.9, f32[8,128,256]{2,1,0:T(8,128)S(1)} %fusion.14, f32[8,1,256]{2,1,0:T(1,128)S(1)} %collective-permute-done.8, f32[8,130,1]{2,1,0:T(8,128)} %copy.32, f32[8,130,258]{2,1,0:T(8,128)} %copy-done.3, ...), kind=kLoop, calls=%fused_computation.9 | loop fusion | flops 3421184 | bytes 5283968 | tf_op jit(solution)/shard_map/mul | solution.py:30
  96.9 15.9 %all_gather.9 = f32[128,1024]{1,0:T(8,128)S(1)} all-gather(f32[128,256]{1,0:T(8,128)S(1)} %add.126), channel_id=1, replica_groups=mesh['gy'=8,'gx'=4] {'gx'}, dimensions={1}, use_global_device_ids=true | all-gather | bytes 655360 | tf_op jit(solution)/shard_map/all_gather | solution.py:97
  113.0 1.9 collective-permute-start.12
  114.9 4.5 %collective-permute-start.13 = (f32[1,1024]{1,0:T(1,128)S(1)}, f32[1,1024]{1,0:T(1,128)S(1)}, u32[]{:S(2)}, u32[]{:S(2)}) collective-permute-start(f32[1,1024]{1,0:T(1,128)S(1)} %get-tuple-element.49), channel_id=1, source_target_pairs={{4,0},{8,4},{12,8},{16,12},{20,16},{24,20},{28,24},{5,1},{9,5},{13... | collective-permute-start | bytes 12296 | tf_op jit(solution)/shard_map/ppermute | solution.py:18
  121.7 2.1 %concatenate.73 = f32[130,1026]{1,0:T(8,128)} concatenate(f32[130,1]{1,0:T(8,128)S(1)} %get-tuple-element.41, f32[130,1024]{1,0:T(8,128)} %copy-done.9, f32[130,1]{1,0:T(8,128)S(1)} %get-tuple-element.40), dimensions={1} | concatenate | bytes 1067040 | tf_op jit(solution)/shard_map/concatenate | solution.py:50
  126.4 15.1 %all-reduce.2 = (f32[]{:T(128)}, f32[]{:T(128)}) all-reduce(f32[]{:T(128)} %get-tuple-element.9, f32[]{:T(128)} %get-tuple-element.8), channel_id=1, replica_groups=mesh['gy'=8,'gx'=4] {'gy'}, use_global_device_ids=true, to_apply=%region_2.3 | all-reduce | flops 2 | bytes 16 | tf_op jit(solution)/shard_map/psum | solution.py:109
  143.1 1.9 collective-permute-start.14
  145.0 4.5 %collective-permute-start.15 = (f32[1,1024]{1,0:T(1,128)S(1)}, f32[1,1024]{1,0:T(1,128)S(1)}, u32[]{:S(2)}, u32[]{:S(2)}) collective-permute-start(f32[1,1024]{1,0:T(1,128)S(1)} %get-tuple-element.47), channel_id=1, source_target_pairs={{4,0},{8,4},{12,8},{16,12},{20,16},{24,20},{28,24},{5,1},{9,5},{13... | collective-permute-start | bytes 12296 | tf_op jit(solution)/shard_map/ppermute | solution.py:18
  151.8 2.1 %concatenate.75 = f32[130,1026]{1,0:T(8,128)} concatenate(f32[130,1]{1,0:T(8,128)S(1)} %get-tuple-element.39, f32[130,1024]{1,0:T(8,128)} %copy-done.10, f32[130,1]{1,0:T(8,128)S(1)} %get-tuple-element.38), dimensions={1} | concatenate | bytes 1067040 | tf_op jit(solution)/shard_map/concatenate | solution.py:50
  155.2 2.2 %multiply_reduce_fusion.2 = (f32[]{:T(128)}, f32[]{:T(128)}, f32[128,1024]{1,0:T(8,128)}) fusion(f32[128,1024]{1,0:T(8,128)S(1)} %copy-done.8, f32[128,1024]{1,0:T(8,128)S(1)} %all_gather.9, f32[128,1024]{1,0:T(8,128)S(1)} %get-tuple-element.19, f32[]{:T(128)S(6)} %div.31, f32[130,1026]{1,0:T(8,128)S(1)} %mul.198, f32[1,130,1024]{2,1,0:T(8,128)S(1)} %copy-done.2, ...), kind=kLoop, calls=%fused_computation.92 | loop fusion | flops 2359294 | bytes 7340044 | tf_op jit(solution)/shard_map/reduce_sum | solution.py:69
  157.4 15.1 %all-reduce.1 = (f32[]{:T(128)}, f32[]{:T(128)}) all-reduce(f32[]{:T(128)} %get-tuple-element.7, f32[]{:T(128)} %get-tuple-element.6), channel_id=1, replica_groups=mesh['gy'=8,'gx'=4] {'gy'}, use_global_device_ids=true, to_apply=%region_6.7 | all-reduce | flops 2 | bytes 16 | tf_op jit(solution)/shard_map/psum | solution.py:109
  177.3 2.1 add_divide_fusion
  180.2 1.9 collective-permute-start.16
  182.1 4.5 %collective-permute-start.17 = (f32[1,1024]{1,0:T(1,128)S(1)}, f32[1,1024]{1,0:T(1,128)S(1)}, u32[]{:S(2)}, u32[]{:S(2)}) collective-permute-start(f32[1,1024]{1,0:T(1,128)S(1)} %get-tuple-element.45), channel_id=1, source_target_pairs={{4,0},{8,4},{12,8},{16,12},{20,16},{24,20},{28,24},{5,1},{9,5},{13... | collective-permute-start | bytes 12296 | tf_op jit(solution)/shard_map/ppermute | solution.py:18
  192.9 15.0 %all-reduce = (f32[]{:T(128)}, f32[]{:T(128)}) all-reduce(f32[]{:T(128)} %get-tuple-element.5, f32[]{:T(128)} %get-tuple-element.4), channel_id=1, replica_groups=mesh['gy'=8,'gx'=4] {'gy'}, use_global_device_ids=true, to_apply=%region_10.11 | all-reduce | flops 2 | bytes 16 | tf_op jit(solution)/shard_map/psum | solution.py:109
  211.9 1.7 fusion.31
  (106 shorter events, 35.7 us)
Async XLA Ops:
  0.6 1.3 copy-start.4
  1.9 3.7 %copy-start = (f32[8,128,256]{2,1,0:T(8,128)S(1)}, f32[8,128,256]{2,1,0:T(8,128)}, u32[]{:S(2)}) copy-start(f32[8,128,256]{2,1,0:T(8,128)} %param.7) | copy-start | bytes 3145732
  1.9 6.4 %copy-start.16 = (f32[128,256]{1,0:T(8,128)S(1)}, f32[128,256]{1,0:T(8,128)}, u32[]{:S(2)}) copy-start(f32[128,256]{1,0:T(8,128)} %param.13) | copy-start | bytes 393220
  2.9 28.0 %collective-permute-start = (f32[3,8,1,256]{3,2,1,0:T(1,128)S(1)}, f32[3,8,1,256]{3,2,1,0:T(1,128)S(1)}, u32[]{:S(2)}, u32[]{:S(2)}) collective-permute-start(f32[3,8,1,256]{3,2,1,0:T(1,128)S(1)} %get-tuple-element.26), channel_id=1, source_target_pairs={{0,4},{4,8},{8,12},{12,16},{16,20},{20,24},{24,28},{28,0},{1,5},{5... | collective-permute-start | bytes 73736 | tf_op jit(solution)/shard_map/ppermute | solution.py:17
  3.0 27.9 %collective-permute-start.1 = (f32[3,8,1,256]{3,2,1,0:T(1,128)S(1)}, f32[3,8,1,256]{3,2,1,0:T(1,128)S(1)}, u32[]{:S(2)}, u32[]{:S(2)}) collective-permute-start(f32[3,8,1,256]{3,2,1,0:T(1,128)S(1)} %get-tuple-element.27), channel_id=1, source_target_pairs={{4,0},{8,4},{12,8},{16,12},{20,16},{24,20},{28,24},{0,28},{5,1},{9... | collective-permute-start | bytes 73736 | tf_op jit(solution)/shard_map/ppermute | solution.py:18
  5.6 18.5 %collective-permute-start.4 = (f32[8,1,256]{2,1,0:T(1,128)S(1)}, f32[8,1,256]{2,1,0:T(1,128)S(1)}, u32[]{:S(2)}, u32[]{:S(2)}) collective-permute-start(f32[8,1,256]{2,1,0:T(1,128)S(1)} %get-tuple-element.35), channel_id=1, source_target_pairs={{0,4},{4,8},{8,12},{12,16},{16,20},{20,24},{24,28},{28,0},{1,5},{5... | collective-permute-start | bytes 24584 | tf_op jit(solution)/shard_map/ppermute | solution.py:17
  5.7 18.5 %collective-permute-start.5 = (f32[8,1,256]{2,1,0:T(1,128)S(1)}, f32[8,1,256]{2,1,0:T(1,128)S(1)}, u32[]{:S(2)}, u32[]{:S(2)}) collective-permute-start(f32[8,1,256]{2,1,0:T(1,128)S(1)} %get-tuple-element.34), channel_id=1, source_target_pairs={{4,0},{8,4},{12,8},{16,12},{20,16},{24,20},{28,24},{0,28},{5,1},{9... | collective-permute-start | bytes 24584 | tf_op jit(solution)/shard_map/ppermute | solution.py:18
  26.7 16.8 %collective-permute-start.6 = (f32[8,130,1]{1,0,2:T(8,128)S(1)}, f32[8,130,1]{1,0,2:T(8,128)S(1)}, u32[]{:S(2)}, u32[]{:S(2)}) collective-permute-start(f32[8,130,1]{1,0,2:T(8,128)S(1)} %copy.27), channel_id=1, source_target_pairs={{0,1},{1,2},{2,3},{3,0},{4,5},{5,6},{6,7},{7,4},{8,9},{9,10},{10,1... | collective-permute-start | bytes 12488 | tf_op jit(solution)/shard_map/ppermute | solution.py:17
  27.8 16.8 %collective-permute-start.7 = (f32[8,130,1]{1,0,2:T(8,128)S(1)}, f32[8,130,1]{1,0,2:T(8,128)S(1)}, u32[]{:S(2)}, u32[]{:S(2)}) collective-permute-start(f32[8,130,1]{1,0,2:T(8,128)S(1)} %copy.29), channel_id=1, source_target_pairs={{1,0},{2,1},{3,2},{0,3},{5,4},{6,5},{7,6},{4,7},{9,8},{10,9},{11,1... | collective-permute-start | bytes 12488 | tf_op jit(solution)/shard_map/ppermute | solution.py:18
  37.3 8.3 %collective-permute-start.2 = (f32[3,8,130,1]{2,1,3,0:T(8,128)S(1)}, f32[3,8,130,1]{2,1,3,0:T(8,128)S(1)}, u32[]{:S(2)}, u32[]{:S(2)}) collective-permute-start(f32[3,8,130,1]{2,1,3,0:T(8,128)S(1)} %copy.23), channel_id=1, source_target_pairs={{0,1},{1,2},{2,3},{3,0},{4,5},{5,6},{6,7},{7,4},{8,9},{9,10},{10,1... | collective-permute-start | bytes 37448 | tf_op jit(solution)/shard_map/ppermute | solution.py:17
  39.7 7.8 %collective-permute-start.3 = (f32[3,8,130,1]{2,1,3,0:T(8,128)S(1)}, f32[3,8,130,1]{2,1,3,0:T(8,128)S(1)}, u32[]{:S(2)}, u32[]{:S(2)}) collective-permute-start(f32[3,8,130,1]{2,1,3,0:T(8,128)S(1)} %copy.24), channel_id=1, source_target_pairs={{1,0},{2,1},{3,2},{0,3},{5,4},{6,5},{7,6},{4,7},{9,8},{10,9},{11,1... | collective-permute-start | bytes 37448 | tf_op jit(solution)/shard_map/ppermute | solution.py:18
  55.2 2.2 %copy-start.3 = (f32[8,130,258]{2,1,0:T(8,128)}, f32[8,130,258]{2,1,0:T(8,128)S(1)}, u32[]{:S(2)}) copy-start(f32[8,130,258]{2,1,0:T(8,128)S(1)} %get-tuple-element.22) | copy-start | bytes 3219844
  56.4 1.2 copy-start.13
  57.6 1.3 copy-start.1
  59.3 19.5 %collective-permute-start.8 = (f32[8,1,256]{2,1,0:T(1,128)S(1)}, f32[8,1,256]{2,1,0:T(1,128)S(1)}, u32[]{:S(2)}, u32[]{:S(2)}) collective-permute-start(f32[8,1,256]{2,1,0:T(1,128)S(1)} %get-tuple-element.33), channel_id=1, source_target_pairs={{0,4},{4,8},{8,12},{12,16},{16,20},{20,24},{24,28},{28,0},{1,5},{5... | collective-permute-start | bytes 24584 | tf_op jit(solution)/shard_map/ppermute | solution.py:17
  59.3 19.5 %collective-permute-start.9 = (f32[8,1,256]{2,1,0:T(1,128)S(1)}, f32[8,1,256]{2,1,0:T(1,128)S(1)}, u32[]{:S(2)}, u32[]{:S(2)}) collective-permute-start(f32[8,1,256]{2,1,0:T(1,128)S(1)} %get-tuple-element.32), channel_id=1, source_target_pairs={{4,0},{8,4},{12,8},{16,12},{20,16},{24,20},{28,24},{0,28},{5,1},{9... | collective-permute-start | bytes 24584 | tf_op jit(solution)/shard_map/ppermute | solution.py:18
  81.5 8.8 %collective-permute-start.10 = (f32[8,130,1]{1,0,2:T(8,128)S(1)}, f32[8,130,1]{1,0,2:T(8,128)S(1)}, u32[]{:S(2)}, u32[]{:S(2)}) collective-permute-start(f32[8,130,1]{1,0,2:T(8,128)S(1)} %copy.31), channel_id=1, source_target_pairs={{0,1},{1,2},{2,3},{3,0},{4,5},{5,6},{6,7},{7,4},{8,9},{9,10},{10,1... | collective-permute-start | bytes 12488 | tf_op jit(solution)/shard_map/ppermute | solution.py:17
  82.9 8.4 %collective-permute-start.11 = (f32[8,130,1]{1,0,2:T(8,128)S(1)}, f32[8,130,1]{1,0,2:T(8,128)S(1)}, u32[]{:S(2)}, u32[]{:S(2)}) collective-permute-start(f32[8,130,1]{1,0,2:T(8,128)S(1)} %copy.33), channel_id=1, source_target_pairs={{1,0},{2,1},{3,2},{0,3},{5,4},{6,5},{7,6},{4,7},{9,8},{10,9},{11,1... | collective-permute-start | bytes 12488 | tf_op jit(solution)/shard_map/ppermute | solution.py:18
  92.4 3.0 %copy-start.5 = (f32[8,129,256]{2,1,0:T(8,128)S(1)}, f32[8,129,256]{2,1,0:T(8,128)}, u32[]{:S(2)}) copy-start(f32[8,129,256]{2,1,0:T(8,128)} %fusion.12) | copy-start | bytes 3170308
  92.4 3.0 %copy-start.15 = (s32[128,256]{1,0:T(8,128)S(1)}, s32[128,256]{1,0:T(8,128)}, u32[]{:S(2)}) copy-start(s32[128,256]{1,0:T(8,128)} %param.10) | copy-start | bytes 393220
  92.4 3.0 %copy-start.18 = (f32[8]{0:T(128)S(1)}, f32[8]{0:T(128)}, u32[]{:S(2)}) copy-start(f32[8]{0:T(128)} %param.11) | copy-start | bytes 100
  95.4 1.5 copy-start.17
  96.9 22.6 %copy-start.2 = (f32[1,130,1024]{2,1,0:T(8,128)S(1)}, f32[1,130,1024]{2,1,0:T(8,128)}, u32[]{:S(2)}) copy-start(f32[1,130,1024]{2,1,0:T(8,128)} %all-gather) | copy-start | bytes 1597444
  113.0 6.9 %collective-permute-start.12 = (f32[1,1024]{1,0:T(1,128)S(1)}, f32[1,1024]{1,0:T(1,128)S(1)}, u32[]{:S(2)}, u32[]{:S(2)}) collective-permute-start(f32[1,1024]{1,0:T(1,128)S(1)} %get-tuple-element.48), channel_id=1, source_target_pairs={{0,4},{4,8},{8,12},{12,16},{16,20},{20,24},{24,28},{1,5},{5,9},{9,... | collective-permute-start | bytes 12296 | tf_op jit(solution)/shard_map/ppermute | solution.py:17
  114.9 5.9 %collective-permute-start.13 = (f32[1,1024]{1,0:T(1,128)S(1)}, f32[1,1024]{1,0:T(1,128)S(1)}, u32[]{:S(2)}, u32[]{:S(2)}) collective-permute-start(f32[1,1024]{1,0:T(1,128)S(1)} %get-tuple-element.49), channel_id=1, source_target_pairs={{4,0},{8,4},{12,8},{16,12},{20,16},{24,20},{28,24},{5,1},{9,5},{13... | collective-permute-start | bytes 12296 | tf_op jit(solution)/shard_map/ppermute | solution.py:18
  143.0 7.8 %copy-start.7 = (f32[128,1024]{1,0:T(8,128)}, f32[128,1024]{1,0:T(8,128)S(1)}, u32[]{:S(2)}) copy-start(f32[128,1024]{1,0:T(8,128)S(1)} %add_divide_fusion.1) | copy-start | bytes 1572868
  143.1 6.5 %collective-permute-start.14 = (f32[1,1024]{1,0:T(1,128)S(1)}, f32[1,1024]{1,0:T(1,128)S(1)}, u32[]{:S(2)}, u32[]{:S(2)}) collective-permute-start(f32[1,1024]{1,0:T(1,128)S(1)} %get-tuple-element.46), channel_id=1, source_target_pairs={{0,4},{4,8},{8,12},{12,16},{16,20},{20,24},{24,28},{1,5},{5,9},{9,... | collective-permute-start | bytes 12296 | tf_op jit(solution)/shard_map/ppermute | solution.py:17
  145.0 5.9 %collective-permute-start.15 = (f32[1,1024]{1,0:T(1,128)S(1)}, f32[1,1024]{1,0:T(1,128)S(1)}, u32[]{:S(2)}, u32[]{:S(2)}) collective-permute-start(f32[1,1024]{1,0:T(1,128)S(1)} %get-tuple-element.47), channel_id=1, source_target_pairs={{4,0},{8,4},{12,8},{16,12},{20,16},{24,20},{28,24},{5,1},{9,5},{13... | collective-permute-start | bytes 12296 | tf_op jit(solution)/shard_map/ppermute | solution.py:18
  153.9 1.2 copy-start.8
  180.2 6.5 %collective-permute-start.16 = (f32[1,1024]{1,0:T(1,128)S(1)}, f32[1,1024]{1,0:T(1,128)S(1)}, u32[]{:S(2)}, u32[]{:S(2)}) collective-permute-start(f32[1,1024]{1,0:T(1,128)S(1)} %get-tuple-element.44), channel_id=1, source_target_pairs={{0,4},{4,8},{8,12},{12,16},{16,20},{20,24},{24,28},{1,5},{5,9},{9,... | collective-permute-start | bytes 12296 | tf_op jit(solution)/shard_map/ppermute | solution.py:17
  182.1 5.9 %collective-permute-start.17 = (f32[1,1024]{1,0:T(1,128)S(1)}, f32[1,1024]{1,0:T(1,128)S(1)}, u32[]{:S(2)}, u32[]{:S(2)}) collective-permute-start(f32[1,1024]{1,0:T(1,128)S(1)} %get-tuple-element.45), channel_id=1, source_target_pairs={{4,0},{8,4},{12,8},{16,12},{20,16},{24,20},{28,24},{5,1},{9,5},{13... | collective-permute-start | bytes 12296 | tf_op jit(solution)/shard_map/ppermute | solution.py:18
  190.3 1.2 copy-start.14
  (5 other events, 4.7 us)
where the time goes:
time: 215 us; the launch traced here: 214 us
  blocking collectives  93.8 us (44%)
  starting transfers between devices  39.2 us (18%)
  other arithmetic  34.3 us (16%)
  local copies, waits for them, and re-layouts  31.6 us (15%)
  between operations  11.2 us (5%)
  waiting for transfers between devices  3.47 us (2%)
    psum x3, blocking collectives, sum_band(): return lax.psum(values, 'gy')  45.2 us
    ppermute x9, starting transfers between devices, extended_2(): after = lax.ppermute(first, axis, down)  32.5 us
    all_gather x1, blocking collectives, on_device(): lax.all_gather(ocean_ext[0, :, 1:-1], 'gx', axis=1, tiled=True)  16.8 us
    all_gather x1, blocking collectives, on_device(): lax.all_gather(forcing, 'gx', axis=1, tiled=True)  15.9 us
    all_gather x1, blocking collectives, on_device(): lax.all_gather(helm, 'gx', axis=1, tiled=True)  15.8 us
    slice x9, local copies, waits for them, and re-layouts, extended_2(): last = lax.slice_in_dim(array, length - width, length, axis=dim)  9.51 us
    concatenate x7, other arithmetic, extended_2(): array = jnp.concatenate([before, array, after], axis=dim)  8.97 us
    ppermute x9, starting transfers between devices, extended_2(): before = lax.ppermute(last, axis, up)  6.72 us
  transfers between devices with their start and end apart: 18, of which 3 were waited for; matrix products, arithmetic and copies ran while one was open for 10% of the time, Pallas kernels for 0%

commit v1 on v0

--- a/solution.py
+++ b/solution.py
@@ -77,6 +77,11 @@
 
 
 def on_device(tracer, east_speed, north_speed, columns, thickness, surface_flux, helm):
+
+    def answer_samples(block_in, pos_dim):
+        res = lax.all_gather(block_in, "gx")
+        return jnp.concatenate(res, axis=pos_dim)
+
     levels, rows_dev, cols_dev = tracer.shape
     depth = lax.broadcasted_iota(jnp.int32, tracer.shape, 0)
     ocean = (depth < columns[None]).astype(jnp.float32)
@@ -96,7 +101,7 @@
     band_rhs, band_helm, band_wet = (
         lax.all_gather(forcing, "gx", axis=1, tiled=True),
         lax.all_gather(helm, "gx", axis=1, tiled=True),
-        lax.all_gather(ocean_ext[0, :, 1:-1], "gx", axis=1, tiled=True),
+        answer_samples(ocean_ext[0, :, 1:-1], 1),
     )
     wet_wrapped = wrap_columns(band_wet)
     band_diagonal = 6.0 + band_helm

time: 215 us -> 223 us (1.037)
  local copies, waits for them, and re-layouts: 31.6 us -> 49.5 us
  blocking collectives: 93.8 us -> 88.6 us
  other arithmetic: 34.3 us -> 32 us
    unnamed x38 -> x58, local copies, waits for them, and re-layouts: 3.82 us -> 14.8 us
    psum x3, blocking collectives: 45.2 us -> 41.9 us  [sum_band(): return lax.psum(values, 'gy')]
    another operation x0 -> x1, local copies, waits for them, and re-layouts: none -> 2.44 us  [on_device(): stacked = jnp.stack([east_speed, north_speed, ocean])]
    concatenate x7 -> x6, other arithmetic: 8.97 us -> 7.59 us  [extended_2(): array = jnp.concatenate([before, array, after], axis=dim)]
  transfers between devices with their start and end apart: 18 -> 18, of which waited for: 3 -> 1; matrix products, arithmetic and copies ran while one was open for 10% -> 14% of each run, Pallas kernels for 0% -> 0%
where the time goes in v1:
time: 223 us; the launch traced here: 221 us
  blocking collectives  88.6 us (40%)
  local copies, waits for them, and re-layouts  49.5 us (22%)
  starting transfers between devices  38.9 us (17%)
  other arithmetic  32 us (14%)
  between operations  10.9 us (5%)
    psum x3, blocking collectives, sum_band(): return lax.psum(values, 'gy')  41.9 us
    ppermute x9, starting transfers between devices, extended_2(): after = lax.ppermute(first, axis, down)  30.4 us
    all_gather x1, blocking collectives, answer_samples(): res = lax.all_gather(block_in, 'gx')  16.1 us
    all_gather x1, blocking collectives, on_device(): lax.all_gather(forcing, 'gx', axis=1, tiled=True)  15.7 us
    all_gather x1, blocking collectives, on_device(): lax.all_gather(helm, 'gx', axis=1, tiled=True)  15 us
    unnamed x58, local copies, waits for them, and re-layouts  14.8 us
    slice x9, local copies, waits for them, and re-layouts, extended_2(): last = lax.slice_in_dim(array, length - width, length, axis=dim)  9.44 us
    ppermute x9, starting transfers between devices, extended_2(): before = lax.ppermute(last, axis, up)  8.53 us
  transfers between devices with their start and end apart: 18, of which 1 were waited for; matrix products, arithmetic and copies ran while one was open for 14% of the time, Pallas kernels for 0%

profile of v1, /device:TPU:4, one launch (start us, length us, event | category | flops | bytes accessed | tf_op | source)
XLA Modules:
  0.0 221.3 jit_solution(2328757100309373554)
XLA Ops:
  1.9 2.4 %copy_bitcast_fusion = (f32[1,8,128,256]{3,1,2,0:T(8,128)S(1)}, f32[1,8,128,256]{3,1,2,0:T(8,128)S(1)}) fusion(f32[8,128,256]{2,1,0:T(8,128)S(1)} %copy-done.21, f32[8,128,256]{2,1,0:T(8,128)} %param.8), kind=kLoop, calls=%fused_computation.43 | loop fusion | bytes 4194304 | tf_op jit(solution)/shard_map/stack | solution.py:88
  5.4 2.6 %collective-permute-start.1 = (f32[3,8,1,256]{3,1,2,0:T(8,128)S(1)}, f32[3,8,1,256]{3,1,2,0:T(8,128)S(1)}, u32[]{:S(2)}, u32[]{:S(2)}) collective-permute-start(f32[3,8,1,256]{3,1,2,0:T(8,128)S(1)} %get-tuple-element.33), channel_id=1, source_target_pairs={{4,0},{8,4},{12,8},{16,12},{20,16},{24,20},{28,24},{0,28},{5,1},{9... | collective-permute-start | bytes 73736 | tf_op jit(solution)/shard_map/ppermute | solution.py:18
  11.4 15.0 %all_gather.10 = f32[128,1024]{1,0:T(8,128)S(1)} all-gather(f32[128,256]{1,0:T(8,128)S(1)} %copy-done.23), channel_id=1, replica_groups=mesh['gy'=8,'gx'=4] {'gx'}, dimensions={1}, use_global_device_ids=true | all-gather | bytes 655360 | tf_op jit(solution)/shard_map/all_gather | solution.py:103
  31.6 2.1 collective-permute-start.6
  34.1 2.0 collective-permute-start.7
  37.6 2.1 fusion.35
  39.7 2.4 %copy.75 = f32[3,8,130,1]{2,1,3,0:T(8,128)S(1)} copy(f32[3,8,130,1]{3,1,2,0:T(8,128)} %get-tuple-element.30) | data formatting | bytes 24960 | tf_op jit(solution)/shard_map/slice | solution.py:15
  42.1 2.4 %copy.76 = f32[3,8,130,1]{2,1,3,0:T(8,128)S(1)} copy(f32[3,8,130,1]{3,1,2,0:T(8,128)} %get-tuple-element.31) | data formatting | bytes 24960 | tf_op jit(solution)/shard_map/slice | solution.py:16
  44.5 4.0 %collective-permute-start.3 = (f32[3,8,130,1]{2,1,3,0:T(8,128)S(1)}, f32[3,8,130,1]{2,1,3,0:T(8,128)S(1)}, u32[]{:S(2)}, u32[]{:S(2)}) collective-permute-start(f32[3,8,130,1]{2,1,3,0:T(8,128)S(1)} %copy.76), channel_id=1, source_target_pairs={{1,0},{2,1},{3,2},{0,3},{5,4},{6,5},{7,6},{4,7},{9,8},{10,9},{11,1... | collective-permute-start | bytes 37448 | tf_op jit(solution)/shard_map/ppermute | solution.py:18
  50.1 2.1 copy.77
  52.2 2.1 copy.78
  54.3 5.9 %pad_maximum_fusion = f32[3,8,130,258]{3,1,2,0:T(8,128)S(1)} fusion(f32[3,8,130,1]{3,1,2,0:T(8,128)} %copy.78, f32[3,8,1,256]{3,1,2,0:T(8,128)S(1)} %collective-permute-done.1, f32[1,8,128,256]{3,1,2,0:T(8,128)S(1)} %fusion.15, f32[1,8,128,256]{3,1,2,0:T(8,128)S(1)} %get-tuple-element.56, f32[1,8,128,256]{3,1,2,0:T(8,128)} %copy-done, ...), kind=kLoop, calls=%fused_computation | loop fusion | flops 4829760 | bytes 6439680 | tf_op jit(solution)/shard_map/concatenate | solution.py:19
  66.4 2.6 %collective-permute-start.9 = (f32[8,1,256]{2,0,1:T(8,128)S(1)}, f32[8,1,256]{2,0,1:T(8,128)S(1)}, u32[]{:S(2)}, u32[]{:S(2)}) collective-permute-start(f32[8,1,256]{2,0,1:T(8,128)S(1)} %get-tuple-element.38), channel_id=1, source_target_pairs={{4,0},{8,4},{12,8},{16,12},{20,16},{24,20},{28,24},{0,28},{5,1},{9... | collective-permute-start | bytes 24584 | tf_op jit(solution)/shard_map/ppermute | solution.py:18
  69.0 16.1 %all_gather.11 = f32[4,130,256]{2,1,0:T(8,128)S(1)} all-gather(f32[1,130,256]{2,1,0:T(8,128)S(1)} %copy.93), channel_id=1, replica_groups=mesh['gy'=8,'gx'=4] {'gx'}, dimensions={0}, use_global_device_ids=true | all-gather | bytes 665600 | tf_op jit(solution)/shard_map/all_gather | solution.py:82
  90.7 3.5 %collective-permute-start.11 = (f32[8,130,1]{1,0,2:T(8,128)S(1)}, f32[8,130,1]{1,0,2:T(8,128)S(1)}, u32[]{:S(2)}, u32[]{:S(2)}) collective-permute-start(f32[8,130,1]{1,0,2:T(8,128)S(1)} %copy.91), channel_id=1, source_target_pairs={{1,0},{2,1},{3,2},{0,3},{5,4},{6,5},{7,6},{4,7},{9,8},{10,9},{11,1... | collective-permute-start | bytes 12488 | tf_op jit(solution)/shard_map/ppermute | solution.py:18
  94.2 3.3 %fusion.12 = f32[8,129,256]{2,0,1:T(8,128)} fusion(f32[8,128,256]{2,0,1:T(8,128)S(1)} %fusion.14, f32[8,1,256]{2,0,1:T(8,128)S(1)} %collective-permute-done.8, f32[8,1,256]{2,0,1:T(8,128)S(1)} %collective-permute-done.9, f32[8,130,258]{2,0,1:T(8,128)} %copy-done.5, f32[8,130,258]{2,0,1:T(8,128)S(1)} %fusion), kind=kLoop, calls=%fused_computation.33 | loop fusion | flops 2377728 | bytes 5292032 | tf_op jit(solution)/shard_map/mul | solution.py:34
  99.9 2.8 %fusion.3 = f32[8,128,257]{2,0,1:T(8,128)S(1)} fusion(f32[8,130,1]{2,0,1:T(8,128)} %copy.92, f32[8,1,256]{2,0,1:T(8,128)S(1)} %collective-permute-done.9, f32[8,128,256]{2,0,1:T(8,128)S(1)} %fusion.14, f32[8,1,256]{2,0,1:T(8,128)S(1)} %collective-permute-done.8, f32[8,130,1]{2,0,1:T(8,128)} %copy.90, f32[8,130,258]{2,0,1:T(8,128)} %copy-done.1, ...), kind=kLoop, calls=%fused_computation.9 | loop fusion | flops 3421184 | bytes 5283968 | tf_op jit(solution)/shard_map/mul | solution.py:30
  104.4 15.7 %all_gather.9 = f32[128,1024]{1,0:T(8,128)S(1)} all-gather(f32[128,256]{1,0:T(8,128)S(1)} %add.126), channel_id=1, replica_groups=mesh['gy'=8,'gx'=4] {'gx'}, dimensions={1}, use_global_device_ids=true | all-gather | bytes 655360 | tf_op jit(solution)/shard_map/all_gather | solution.py:102
  120.2 1.9 collective-permute-start.12
  122.1 4.8 %collective-permute-start.13 = (f32[1,1024]{1,0:T(1,128)S(1)}, f32[1,1024]{1,0:T(1,128)S(1)}, u32[]{:S(2)}, u32[]{:S(2)}) collective-permute-start(f32[1,1024]{1,0:T(1,128)S(1)} %get-tuple-element.55), channel_id=1, source_target_pairs={{4,0},{8,4},{12,8},{16,12},{20,16},{24,20},{28,24},{5,1},{9,5},{13... | collective-permute-start | bytes 12296 | tf_op jit(solution)/shard_map/ppermute | solution.py:18
  131.1 2.1 concatenate.73
  135.7 13.0 %all-reduce.2 = (f32[]{:T(128)}, f32[]{:T(128)}) all-reduce(f32[]{:T(128)} %get-tuple-element.15, f32[]{:T(128)} %get-tuple-element.14), channel_id=1, replica_groups=mesh['gy'=8,'gx'=4] {'gy'}, use_global_device_ids=true, to_apply=%region_2.3 | all-reduce | flops 2 | bytes 16 | tf_op jit(solution)/shard_map/psum | solution.py:114
  152.1 4.5 %collective-permute-start.15 = (f32[1,1024]{1,0:T(1,128)S(1)}, f32[1,1024]{1,0:T(1,128)S(1)}, u32[]{:S(2)}, u32[]{:S(2)}) collective-permute-start(f32[1,1024]{1,0:T(1,128)S(1)} %get-tuple-element.53), channel_id=1, source_target_pairs={{4,0},{8,4},{12,8},{16,12},{20,16},{24,20},{28,24},{5,1},{9,5},{13... | collective-permute-start | bytes 12296 | tf_op jit(solution)/shard_map/ppermute | solution.py:18
  159.0 2.1 concatenate.75
  162.3 2.2 %multiply_reduce_fusion.2 = (f32[]{:T(128)}, f32[]{:T(128)}, f32[128,1024]{1,0:T(8,128)}) fusion(f32[128,1024]{1,0:T(8,128)S(1)} %copy-done.7, f32[128,1024]{1,0:T(8,128)S(1)} %all_gather.9, f32[128,1024]{1,0:T(8,128)S(1)} %get-tuple-element.25, f32[]{:T(128)S(6)} %div.31, f32[128,1024]{1,0:T(8,128)S(1)} %copy.96, f32[130,1026]{1,0:T(8,128)S(1)} %mul.198, ...), kind=kLoop, calls=%fused_computation.88 | loop fusion | flops 2359294 | bytes 7340044 | tf_op jit(solution)/shard_map/reduce_sum | solution.py:69
  164.6 15.1 %all-reduce.1 = (f32[]{:T(128)}, f32[]{:T(128)}) all-reduce(f32[]{:T(128)} %get-tuple-element.13, f32[]{:T(128)} %get-tuple-element.12), channel_id=1, replica_groups=mesh['gy'=8,'gx'=4] {'gy'}, use_global_device_ids=true, to_apply=%region_6.7 | all-reduce | flops 2 | bytes 16 | tf_op jit(solution)/shard_map/psum | solution.py:114
  184.1 2.1 add_divide_fusion
  187.0 2.1 collective-permute-start.16
  189.0 4.5 %collective-permute-start.17 = (f32[1,1024]{1,0:T(1,128)S(1)}, f32[1,1024]{1,0:T(1,128)S(1)}, u32[]{:S(2)}, u32[]{:S(2)}) collective-permute-start(f32[1,1024]{1,0:T(1,128)S(1)} %get-tuple-element.51), channel_id=1, source_target_pairs={{4,0},{8,4},{12,8},{16,12},{20,16},{24,20},{28,24},{5,1},{9,5},{13... | collective-permute-start | bytes 12296 | tf_op jit(solution)/shard_map/ppermute | solution.py:18
  193.6 2.5 %copy.99 = f32[8,128,256]{2,1,0:T(8,128)} copy(f32[8,128,256]{2,0,1:T(8,128)} %get-tuple-element.27) | data formatting | bytes 2097152
  197.1 2.2 concatenate.77
  202.0 13.8 %all-reduce = (f32[]{:T(128)}, f32[]{:T(128)}) all-reduce(f32[]{:T(128)} %get-tuple-element.11, f32[]{:T(128)} %get-tuple-element.10), channel_id=1, replica_groups=mesh['gy'=8,'gx'=4] {'gy'}, use_global_device_ids=true, to_apply=%region_10.11 | all-reduce | flops 2 | bytes 16 | tf_op jit(solution)/shard_map/psum | solution.py:114
  (132 shorter events, 48.3 us)
Async XLA Ops:
  0.6 1.3 copy-start.21
  4.4 3.7 %copy-start.2 = (f32[8,128,256]{2,1,0:T(8,128)S(1)}, f32[8,128,256]{2,1,0:T(8,128)}, u32[]{:S(2)}) copy-start(f32[8,128,256]{2,1,0:T(8,128)} %param.7) | copy-start | bytes 3145732
  5.4 6.0 %copy-start.23 = (f32[128,256]{1,0:T(8,128)S(1)}, f32[128,256]{1,0:T(8,128)}, u32[]{:S(2)}) copy-start(f32[128,256]{1,0:T(8,128)} %param.13) | copy-start | bytes 393220
  5.4 30.7 %collective-permute-start = (f32[3,8,1,256]{3,1,2,0:T(8,128)S(1)}, f32[3,8,1,256]{3,1,2,0:T(8,128)S(1)}, u32[]{:S(2)}, u32[]{:S(2)}) collective-permute-start(f32[3,8,1,256]{3,1,2,0:T(8,128)S(1)} %get-tuple-element.32), channel_id=1, source_target_pairs={{0,4},{4,8},{8,12},{12,16},{16,20},{20,24},{24,28},{28,0},{1,5},{5... | collective-permute-start | bytes 73736 | tf_op jit(solution)/shard_map/ppermute | solution.py:17
  5.4 30.7 %collective-permute-start.1 = (f32[3,8,1,256]{3,1,2,0:T(8,128)S(1)}, f32[3,8,1,256]{3,1,2,0:T(8,128)S(1)}, u32[]{:S(2)}, u32[]{:S(2)}) collective-permute-start(f32[3,8,1,256]{3,1,2,0:T(8,128)S(1)} %get-tuple-element.33), channel_id=1, source_target_pairs={{4,0},{8,4},{12,8},{16,12},{20,16},{24,20},{28,24},{0,28},{5,1},{9... | collective-permute-start | bytes 73736 | tf_op jit(solution)/shard_map/ppermute | solution.py:18
  8.7 17.7 %collective-permute-start.4 = (f32[8,1,256]{2,0,1:T(8,128)S(1)}, f32[8,1,256]{2,0,1:T(8,128)S(1)}, u32[]{:S(2)}, u32[]{:S(2)}) collective-permute-start(f32[8,1,256]{2,0,1:T(8,128)S(1)} %get-tuple-element.41), channel_id=1, source_target_pairs={{0,4},{4,8},{8,12},{12,16},{16,20},{20,24},{24,28},{28,0},{1,5},{5... | collective-permute-start | bytes 24584 | tf_op jit(solution)/shard_map/ppermute | solution.py:17
  9.6 18.6 %collective-permute-start.5 = (f32[8,1,256]{2,0,1:T(8,128)S(1)}, f32[8,1,256]{2,0,1:T(8,128)S(1)}, u32[]{:S(2)}, u32[]{:S(2)}) collective-permute-start(f32[8,1,256]{2,0,1:T(8,128)S(1)} %get-tuple-element.40), channel_id=1, source_target_pairs={{4,0},{8,4},{12,8},{16,12},{20,16},{24,20},{28,24},{0,28},{5,1},{9... | collective-permute-start | bytes 24584 | tf_op jit(solution)/shard_map/ppermute | solution.py:18
  31.6 16.9 %collective-permute-start.6 = (f32[8,130,1]{1,0,2:T(8,128)S(1)}, f32[8,130,1]{1,0,2:T(8,128)S(1)}, u32[]{:S(2)}, u32[]{:S(2)}) collective-permute-start(f32[8,130,1]{1,0,2:T(8,128)S(1)} %copy.82), channel_id=1, source_target_pairs={{0,1},{1,2},{2,3},{3,0},{4,5},{5,6},{6,7},{7,4},{8,9},{9,10},{10,1... | collective-permute-start | bytes 12488 | tf_op jit(solution)/shard_map/ppermute | solution.py:17
  34.1 14.9 %collective-permute-start.7 = (f32[8,130,1]{1,0,2:T(8,128)S(1)}, f32[8,130,1]{1,0,2:T(8,128)S(1)}, u32[]{:S(2)}, u32[]{:S(2)}) collective-permute-start(f32[8,130,1]{1,0,2:T(8,128)S(1)} %copy.84), channel_id=1, source_target_pairs={{1,0},{2,1},{3,2},{0,3},{5,4},{6,5},{7,6},{4,7},{9,8},{10,9},{11,1... | collective-permute-start | bytes 12488 | tf_op jit(solution)/shard_map/ppermute | solution.py:18
  42.1 8.0 %collective-permute-start.2 = (f32[3,8,130,1]{2,1,3,0:T(8,128)S(1)}, f32[3,8,130,1]{2,1,3,0:T(8,128)S(1)}, u32[]{:S(2)}, u32[]{:S(2)}) collective-permute-start(f32[3,8,130,1]{2,1,3,0:T(8,128)S(1)} %copy.75), channel_id=1, source_target_pairs={{0,1},{1,2},{2,3},{3,0},{4,5},{5,6},{6,7},{7,4},{8,9},{9,10},{10,1... | collective-permute-start | bytes 37448 | tf_op jit(solution)/shard_map/ppermute | solution.py:17
  44.5 7.7 %collective-permute-start.3 = (f32[3,8,130,1]{2,1,3,0:T(8,128)S(1)}, f32[3,8,130,1]{2,1,3,0:T(8,128)S(1)}, u32[]{:S(2)}, u32[]{:S(2)}) collective-permute-start(f32[3,8,130,1]{2,1,3,0:T(8,128)S(1)} %copy.76), channel_id=1, source_target_pairs={{1,0},{2,1},{3,2},{0,3},{5,4},{6,5},{7,6},{4,7},{9,8},{10,9},{11,1... | collective-permute-start | bytes 37448 | tf_op jit(solution)/shard_map/ppermute | solution.py:18
  60.4 3.6 %copy-start.5 = (f32[8,130,258]{2,0,1:T(8,128)}, f32[8,130,258]{2,0,1:T(8,128)S(1)}, u32[]{:S(2)}) copy-start(f32[8,130,258]{2,0,1:T(8,128)S(1)} %get-tuple-element.29) | copy-start | bytes 3219844
  60.5 2.0 copy-start.11
  60.5 2.5 %copy-start.19 = (f32[8,130,1]{2,0,1:T(8,128)S(1)}, f32[8,130,1]{2,0,1:T(8,128)}, u32[]{:S(2)}) copy-start(f32[8,130,1]{2,0,1:T(8,128)} %copy.85) | copy-start | bytes 12484
  66.3 20.0 %collective-permute-start.8 = (f32[8,1,256]{2,0,1:T(8,128)S(1)}, f32[8,1,256]{2,0,1:T(8,128)S(1)}, u32[]{:S(2)}, u32[]{:S(2)}) collective-permute-start(f32[8,1,256]{2,0,1:T(8,128)S(1)} %get-tuple-element.39), channel_id=1, source_target_pairs={{0,4},{4,8},{8,12},{12,16},{16,20},{20,24},{24,28},{28,0},{1,5},{5... | collective-permute-start | bytes 24584 | tf_op jit(solution)/shard_map/ppermute | solution.py:17
  66.4 19.9 %collective-permute-start.9 = (f32[8,1,256]{2,0,1:T(8,128)S(1)}, f32[8,1,256]{2,0,1:T(8,128)S(1)}, u32[]{:S(2)}, u32[]{:S(2)}) collective-permute-start(f32[8,1,256]{2,0,1:T(8,128)S(1)} %get-tuple-element.38), channel_id=1, source_target_pairs={{4,0},{8,4},{12,8},{16,12},{20,16},{24,20},{28,24},{0,28},{5,1},{9... | collective-permute-start | bytes 24584 | tf_op jit(solution)/shard_map/ppermute | solution.py:18
  88.9 8.6 %collective-permute-start.10 = (f32[8,130,1]{1,0,2:T(8,128)S(1)}, f32[8,130,1]{1,0,2:T(8,128)S(1)}, u32[]{:S(2)}, u32[]{:S(2)}) collective-permute-start(f32[8,130,1]{1,0,2:T(8,128)S(1)} %copy.89), channel_id=1, source_target_pairs={{0,1},{1,2},{2,3},{3,0},{4,5},{5,6},{6,7},{7,4},{8,9},{9,10},{10,1... | collective-permute-start | bytes 12488 | tf_op jit(solution)/shard_map/ppermute | solution.py:17
  90.7 8.0 %collective-permute-start.11 = (f32[8,130,1]{1,0,2:T(8,128)S(1)}, f32[8,130,1]{1,0,2:T(8,128)S(1)}, u32[]{:S(2)}, u32[]{:S(2)}) collective-permute-start(f32[8,130,1]{1,0,2:T(8,128)S(1)} %copy.91), channel_id=1, source_target_pairs={{1,0},{2,1},{3,2},{0,3},{5,4},{6,5},{7,6},{4,7},{9,8},{10,9},{11,1... | collective-permute-start | bytes 12488 | tf_op jit(solution)/shard_map/ppermute | solution.py:18
  99.9 2.8 %copy-start.4 = (f32[8,129,256]{2,0,1:T(8,128)S(1)}, f32[8,129,256]{2,0,1:T(8,128)}, u32[]{:S(2)}) copy-start(f32[8,129,256]{2,0,1:T(8,128)} %fusion.12) | copy-start | bytes 3170308
  99.9 2.8 %copy-start.22 = (s32[128,256]{1,0:T(8,128)S(1)}, s32[128,256]{1,0:T(8,128)}, u32[]{:S(2)}) copy-start(s32[128,256]{1,0:T(8,128)} %param.10) | copy-start | bytes 393220
  99.9 2.8 %copy-start.25 = (f32[8]{0:T(128)S(1)}, f32[8]{0:T(128)}, u32[]{:S(2)}) copy-start(f32[8]{0:T(128)} %param.11) | copy-start | bytes 100
  102.7 1.6 copy-start.24
  104.4 23.5 %copy-start.9 = (f32[4,130,256]{2,1,0:T(8,128)S(1)}, f32[4,130,256]{2,1,0:T(8,128)}, u32[]{:S(2)}) copy-start(f32[4,130,256]{2,1,0:T(8,128)} %copy-done.8) | copy-start | bytes 1597444
  120.2 9.9 %collective-permute-start.12 = (f32[1,1024]{1,0:T(1,128)S(1)}, f32[1,1024]{1,0:T(1,128)S(1)}, u32[]{:S(2)}, u32[]{:S(2)}) collective-permute-start(f32[1,1024]{1,0:T(1,128)S(1)} %get-tuple-element.54), channel_id=1, source_target_pairs={{0,4},{4,8},{8,12},{12,16},{16,20},{20,24},{24,28},{1,5},{5,9},{9,... | collective-permute-start | bytes 12296 | tf_op jit(solution)/shard_map/ppermute | solution.py:17
  122.1 8.0 %collective-permute-start.13 = (f32[1,1024]{1,0:T(1,128)S(1)}, f32[1,1024]{1,0:T(1,128)S(1)}, u32[]{:S(2)}, u32[]{:S(2)}) collective-permute-start(f32[1,1024]{1,0:T(1,128)S(1)} %get-tuple-element.55), channel_id=1, source_target_pairs={{4,0},{8,4},{12,8},{16,12},{20,16},{24,20},{28,24},{5,1},{9,5},{13... | collective-permute-start | bytes 12296 | tf_op jit(solution)/shard_map/ppermute | solution.py:18
  150.2 7.8 %copy-start.6 = (f32[128,1024]{1,0:T(8,128)}, f32[128,1024]{1,0:T(8,128)S(1)}, u32[]{:S(2)}) copy-start(f32[128,1024]{1,0:T(8,128)S(1)} %add_divide_fusion.1) | copy-start | bytes 1572868
  150.2 6.5 %collective-permute-start.14 = (f32[1,1024]{1,0:T(1,128)S(1)}, f32[1,1024]{1,0:T(1,128)S(1)}, u32[]{:S(2)}, u32[]{:S(2)}) collective-permute-start(f32[1,1024]{1,0:T(1,128)S(1)} %get-tuple-element.52), channel_id=1, source_target_pairs={{0,4},{4,8},{8,12},{12,16},{16,20},{20,24},{24,28},{1,5},{5,9},{9,... | collective-permute-start | bytes 12296 | tf_op jit(solution)/shard_map/ppermute | solution.py:17
  152.1 5.9 %collective-permute-start.15 = (f32[1,1024]{1,0:T(1,128)S(1)}, f32[1,1024]{1,0:T(1,128)S(1)}, u32[]{:S(2)}, u32[]{:S(2)}) collective-permute-start(f32[1,1024]{1,0:T(1,128)S(1)} %get-tuple-element.53), channel_id=1, source_target_pairs={{4,0},{8,4},{12,8},{16,12},{20,16},{24,20},{28,24},{5,1},{9,5},{13... | collective-permute-start | bytes 12296 | tf_op jit(solution)/shard_map/ppermute | solution.py:18
  186.9 9.2 %copy-start.18 = (f32[128,1024]{1,0:T(8,128)S(1)}, f32[128,1024]{1,0:T(8,128)}, u32[]{:S(2)}) copy-start(f32[128,1024]{1,0:T(8,128)} %copy-done.17) | copy-start | bytes 1572868
  187.0 9.2 %collective-permute-start.16 = (f32[1,1024]{1,0:T(1,128)S(1)}, f32[1,1024]{1,0:T(1,128)S(1)}, u32[]{:S(2)}, u32[]{:S(2)}) collective-permute-start(f32[1,1024]{1,0:T(1,128)S(1)} %get-tuple-element.50), channel_id=1, source_target_pairs={{0,4},{4,8},{8,12},{12,16},{16,20},{20,24},{24,28},{1,5},{5,9},{9,... | collective-permute-start | bytes 12296 | tf_op jit(solution)/shard_map/ppermute | solution.py:17
  189.0 7.1 %collective-permute-start.17 = (f32[1,1024]{1,0:T(1,128)S(1)}, f32[1,1024]{1,0:T(1,128)S(1)}, u32[]{:S(2)}, u32[]{:S(2)}) collective-permute-start(f32[1,1024]{1,0:T(1,128)S(1)} %get-tuple-element.51), channel_id=1, source_target_pairs={{4,0},{8,4},{12,8},{16,12},{20,16},{24,20},{28,24},{5,1},{9,5},{13... | collective-permute-start | bytes 12296 | tf_op jit(solution)/shard_map/ppermute | solution.py:18
  197.1 3.3 %copy-start.20 = (f32[128,1024]{1,0:T(8,128)S(1)}, f32[128,1024]{1,0:T(8,128)}, u32[]{:S(2)}) copy-start(f32[128,1024]{1,0:T(8,128)} %get-tuple-element.23) | copy-start | bytes 1572868
  (12 other events, 12.4 us)
